TPU v7x, 256 devices: a whole 4x4x8 slice. The times are simulated.
256 devices in a mesh: atom: 32 (over x, z_lo, core), chan: 8 (over y, z_hi).
Axes of the slice: x: 4, y: 4, z: 8 (z_hi: 2, z_lo: 4; z = z_hi * 4 + z_lo), core: 2. Of those that a mesh axis runs over, the one named last changes fastest.
Arguments:
- positions: float32 [3, 4096], P(None, 'atom'), may hold values from -9 to 9
- features: bfloat16 [512, 4096], P('chan', 'atom'), may hold values from -6 to 6
- struct_ids: int32 [4096], P('atom'), may hold values from 0 to 31, as said below
- slots: int32 [64, 4096], P(None, 'atom'), may hold values from 0 to 96, as said below
- validity: int32 [64, 4096], P(None, 'atom'), may hold values from 0 to 1, as said below
- radial_in: bfloat16 [512, 128], replicated, may hold values from -72 to 72
- radial_out: bfloat16 [512, 512], P('chan'), may hold values from -0.0234375 to 0.0234375
- mixing: bfloat16 [512, 512], P(None, 'chan'), may hold values from -0.5 to 0.5
- readout: float32 [512], replicated, may hold values from -0.0078125 to 0.0078125
Outputs:
- forces: float32 [3, 4096], P(None, 'atom')
- stress: float32 [9, 32], replicated
Inputs may be any that keep to these rules, and one draw needn't show every extreme that they name: `struct_ids`: structure numbers never fall along the atoms and every structure has at least one atom. `slots`: the 64 slot values of one atom are distinct and never equal 48. `validity`: an edge is valid only where its neighbour atom exists and belongs to the same structure.
All inputs are finite; a program needn't handle non-finite values.
Results may differ from a plain program's by a relative error of at most 0.0099.
Values may be sent and summed in bfloat16 or wider, within the bound.
No kernel may reach another device: no remote copies, remote signals or barrier semaphores. Data moves between devices by JAX's collectives and lax.ppermute only.
A program may use at most 64 MiB of HBM per device.

v0:
```python
import jax
import jax.numpy as jnp
from jax import lax
from jax.sharding import PartitionSpec as P

RIM = 48
sharpness = 40.0
reach = 10.0


def with_halo(value, sides, width):
    for axis, dim in sides:
        size, length = (lax.axis_size(axis), value.shape[dim])
        up = [(i, (i + 1) % size) for i in range(size - 1)]
        down = [(j, i) for i, j in up]
        last = lax.slice_in_dim(value, length - width, length, axis=dim)
        first = lax.slice_in_dim(value, 0, width, axis=dim)
        before = lax.ppermute(last, axis, up)
        after = lax.ppermute(first, axis, down)
        value = jnp.concatenate([before, value, after], axis=dim)
    return value


def turned_gather(arrays, axis, dims):
    turned = [jnp.moveaxis(a, dim, 0) for a, dim in zip(arrays, dims)]
    both = jnp.concatenate([t.reshape(len(t), -1) for t in turned], axis=1)
    result, at, outs = (lax.all_gather(both, axis, axis=0, tiled=True), 0, [])
    for t, dim in zip(turned, dims):
        share = result[:, at : at + t[0].size].reshape(-1, *t.shape[1:])
        outs.append(jnp.moveaxis(share, 0, dim))
        at += t[0].size
    return tuple(outs)


def sent_to_all(value, axis):
    copies = jnp.broadcast_to(value, (lax.axis_size(axis), *value.shape))
    return lax.all_to_all(copies, axis, split_axis=0, concat_axis=0, tiled=True)


def of_everyone(value, axis):
    everything = sent_to_all(value, axis)
    return jnp.sum(everything, axis=0)


def packed_total(arrays, axis):
    flat, at, outs = (jnp.concatenate([a.reshape(-1) for a in arrays]), 0, [])
    running = of_everyone(flat, axis)
    for a in arrays:
        outs.append(running[at : at + a.size].reshape(a.shape))
        at += a.size
    return tuple(outs)


def from_behind(value, axis, by):
    size = lax.axis_size(axis)
    pairs = [(i, i + by) for i in range(size) if 0 <= i + by < size]
    return lax.ppermute(value, axis, pairs)


def dsilu(value):
    sigma = jax.nn.sigmoid(value)
    return sigma * (1.0 + value * (1.0 - sigma))


def radial_terms(vector, radial_in, radial_out):
    dist = jnp.sqrt(1.0 + jnp.sum(vector * vector, axis=0))
    count = radial_in.shape[1]
    centers = jnp.arange(count).astype(jnp.float32) * (reach / count)
    offset = dist[None, :] - centers[:, None]
    bump = jnp.exp(-sharpness * offset * offset)
    basis = bump.astype(jnp.bfloat16)
    slope = (-2.0 * sharpness * offset * bump).astype(jnp.bfloat16)
    pre = jnp.dot(radial_in, basis, preferred_element_type=jnp.float32)
    dpre = jnp.dot(radial_in, slope, preferred_element_type=jnp.float32)
    hidden = jax.nn.silu(pre).astype(jnp.bfloat16)
    dhidden = (dsilu(pre) * dpre).astype(jnp.bfloat16)
    radial = jnp.dot(radial_out, hidden, preferred_element_type=jnp.float32)
    dradial = jnp.dot(radial_out, dhidden, preferred_element_type=jnp.float32)
    return (dist, radial, dradial)


def local(positions, features, struct_ids, slots, validity, radial_in, radial_out, mixing, readout):
    slot_count, atom_count = slots.shape
    padded_feat, padded_pos = (
        with_halo(features.astype(jnp.float32), (("atom", 1),), RIM).astype(features.dtype),
        with_halo(positions, (("atom", 1),), RIM),
    )
    atom_index = jnp.arange(atom_count, dtype=jnp.int32)
    whole_feat, whole_radial, whole_mix = turned_gather(
        (padded_feat, radial_out, mixing), "chan", (0, 0, 1)
    )
    used = slot_count // lax.axis_size("chan")
    first = lax.axis_index("chan") * used
    slot_rows = lax.dynamic_slice_in_dim(slots, first, used, 0)
    valid_rows = lax.dynamic_slice_in_dim(validity, first, used, 0)
    flat_index = (atom_index[None, :] + slot_rows).reshape(-1)
    far_feat = whole_feat[:, flat_index]
    vector = padded_pos[:, flat_index] - jnp.tile(positions, (1, used))
    weight = valid_rows.reshape(-1).astype(jnp.float32)
    dist, radial, dradial = radial_terms(vector, radial_in, whole_radial)
    message = (far_feat * radial).astype(jnp.bfloat16)
    mixed = jnp.dot(whole_mix, message, preferred_element_type=jnp.float32)
    gmix = (weight[None, :] * readout[:, None] * dsilu(mixed)).astype(jnp.bfloat16)
    gmsg = lax.dot_general(
        whole_mix, gmix, (((0,), (0,)), ((), ())), preferred_element_type=jnp.float32
    )
    gdist = jnp.sum(gmsg * far_feat.astype(jnp.float32) * dradial, axis=0)
    gvec = gdist * vector / dist
    outgoing = gvec.reshape(3, used, atom_count).sum(axis=1)
    table = jnp.zeros((3, atom_count + 2 * RIM), jnp.float32).at[:, flat_index].add(-gvec)
    table = table.at[:, RIM : RIM + atom_count].add(outgoing)
    atomvir = (vector[:, None, :] * gvec[None, :, :]).reshape(9, used, atom_count).sum(axis=1)
    table, atomvir = packed_total((table, atomvir), "chan")
    from_next = from_behind(table[:, :RIM], "atom", -1)
    from_prior = from_behind(table[:, RIM + atom_count :], "atom", 1)
    forces = table[:, RIM : RIM + atom_count]
    forces = forces + jnp.pad(from_prior, ((0, 0), (0, atom_count - RIM)))
    forces = forces + jnp.pad(from_next, ((0, 0), (atom_count - RIM, 0)))
    struct_total = atom_count * lax.axis_size("atom") // 128
    onehot = (struct_ids[None, :] == jnp.arange(struct_total, dtype=jnp.int32)[:, None]).astype(
        jnp.float32
    )
    virial = jnp.dot(atomvir, onehot.T, precision=lax.Precision.HIGHEST)
    counts = jnp.sum(onehot, axis=1)
    virial, counts = packed_total((virial, counts), "atom")
    stress = -virial / counts[None, :]
    return (forces, stress)


def solution(mesh):
    placed = (
        P(None, "atom"),
        P("chan", "atom"),
        P("atom"),
        P(None, "atom"),
        P(None, "atom"),
        P(),
        P("chan", None),
        P(None, "chan"),
        P(),
    )
    return jax.shard_map(
        local, mesh=mesh, in_specs=placed, out_specs=(P(None, "atom"), P()), check_vma=False
    )
```

profile of v0, /device:TPU:1, one launch (start us, length us, event | category | flops | bytes accessed | tf_op | source)
XLA Modules:
  0.0 156.5 jit_solution(10200751247860224397)
XLA Ops:
  7.2 0.9 fusion.56
  8.1 4.9 %collective-permute-start = (bf16[64,48]{1,0:T(8,128)(2,1)S(1)}, bf16[64,48]{1,0:T(8,128)(2,1)S(1)}, u32[]{:S(2)}, u32[]{:S(2)}) collective-permute-start(bf16[64,48]{1,0:T(8,128)(2,1)S(1)} %get-tuple-element.19), channel_id=1, source_target_pairs={{0,8},{8,16},{16,24},{24,32},{32,40},{40,48},{48,56},{56,64},{64,7... | collective-permute-start | bytes 18440 | tf_op jit(solution)/shard_map/ppermute | solution.py:18
  13.0 1.9 %collective-permute-start.1 = (bf16[64,48]{1,0:T(8,128)(2,1)S(1)}, bf16[64,48]{1,0:T(8,128)(2,1)S(1)}, u32[]{:S(2)}, u32[]{:S(2)}) collective-permute-start(bf16[64,48]{1,0:T(8,128)(2,1)S(1)} %get-tuple-element.18), channel_id=1, source_target_pairs={{8,0},{16,8},{24,16},{32,24},{40,32},{48,40},{56,48},{64,56},{72,6... | collective-permute-start | bytes 18440 | tf_op jit(solution)/shard_map/ppermute | solution.py:19
  15.0 3.1 %collective-permute-done.1 = bf16[64,48]{1,0:T(8,128)(2,1)S(1)} collective-permute-done((bf16[64,48]{1,0:T(8,128)(2,1)S(1)}, bf16[64,48]{1,0:T(8,128)(2,1)S(1)}, u32[]{:S(2)}, u32[]{:S(2)}) %collective-permute-start.1) | collective-permute-done | bytes 6176 | tf_op jit(solution)/shard_map/ppermute | solution.py:19
  18.1 1.7 %concatenate.17 = bf16[64,1248]{1,0:T(8,128)(2,1)} concatenate(bf16[64,48]{1,0:T(8,128)(2,1)S(1)} %collective-permute-done, bf16[64,128]{1,0:T(8,128)(2,1)} %param.12, bf16[64,48]{1,0:T(8,128)(2,1)S(1)} %collective-permute-done.1, bf16[64,512]{1,0:T(8,128)(2,1)} %param.17, bf16[64,512]{1,0:T(8,128)(2,1)} %bitcast.80), dimensions={1} | concatenate | bytes 319488 | tf_op jit(solution)/shard_map/concatenate | solution.py:26
  19.8 0.8 fusion.58
  20.6 1.9 %collective-permute-start.3 = (f32[3,48]{1,0:T(4,128)S(1)}, f32[3,48]{1,0:T(4,128)S(1)}, u32[]{:S(2)}, u32[]{:S(2)}) collective-permute-start(f32[3,48]{1,0:T(4,128)S(1)} %get-tuple-element.25), channel_id=1, source_target_pairs={{8,0},{16,8},{24,16},{32,24},{40,32},{48,40},{56,48},{64,56},{72,6... | collective-permute-start | bytes 1736 | tf_op jit(solution)/shard_map/ppermute | solution.py:19
  22.6 3.6 %collective-permute-start.2 = (f32[3,48]{1,0:T(4,128)S(1)}, f32[3,48]{1,0:T(4,128)S(1)}, u32[]{:S(2)}, u32[]{:S(2)}) collective-permute-start(f32[3,48]{1,0:T(4,128)S(1)} %get-tuple-element.24), channel_id=1, source_target_pairs={{0,8},{8,16},{16,24},{24,32},{32,40},{40,48},{48,56},{56,64},{64,7... | collective-permute-start | bytes 1736 | tf_op jit(solution)/shard_map/ppermute | solution.py:18
  26.2 0.7 dynamic-slice_add_fusion
  26.9 1.3 convert_bitcast_fusion
  28.2 0.7 broadcast_bitcast_fusion
  28.9 0.7 compare_reduce_fusion
  29.6 0.8 pad_maximum_fusion.1
  30.5 2.8 %gather_fusion.1 = f32[1024,3]{1,0:T(8,128)S(1)} fusion(f32[3,224]{0,1:T(8,128)S(1)} %copy.79, s32[1024]{0:T(1024)S(1)} %broadcast_clamp_fusion), kind=kCustom, calls=%fused_computation.1 | custom fusion | bytes 28672 | tf_op jit(solution)/shard_map/gather | solution.py:98
  34.2 52.5 %all-gather.2.cloned.1.call-done = bf16[512,1248]{1,0:T(8,128)(2,1)} async-done(((bf16[64,1248]{1,0:T(8,128)(2,1)}), bf16[512,1248]{1,0:T(8,128)(2,1)}) %all-gather.2.cloned.1.call-update) | async-done | bytes 1277968 | tf_op jit(solution)/shard_map/all_gather | solution.py:27
  86.7 1.0 slice.91
  87.8 4.0 %gather_fusion = bf16[1024,512]{1,0:T(8,128)(2,1)S(1)} fusion(bf16[512,224]{0,1:T(8,128)(2,1)S(1)} %copy.91, s32[1024]{0:T(1024)S(1)} %broadcast_clamp_fusion), kind=kCustom, calls=%fused_computation | custom fusion | bytes 2101248 | tf_op jit(solution)/shard_map/gather | solution.py:97
  91.8 1.3 copy.78
  93.1 3.6 %multiply_convert_fusion = bf16[512,1024]{0,1:T(8,128)(2,1)S(1)} fusion(bf16[1024,512]{0,1:T(8,128)(2,1)} %copy.78, f32[1024,512]{1,0:T(8,128)S(1)} %fusion.25, f32[512]{0:T(512)S(1)} %copy-done.7, f32[1024]{0:T(1024)S(1)} %copy-done.3, bf16[512,1248]{1,0:T(8,128)(2,1)} %all-gather.2.cloned.1.call-done), kind=kOutput, calls=%fused_computation.19 | convolution fusion | flops 1083179008 | bytes 5249024 | tf_op jit(solution)/shard_map/dot_general | solution.py:102
  96.8 1.9 %fusion.20 = f32[512,1024]{1,0:T(8,128)S(1)} fusion(bf16[512,1024]{0,1:T(8,128)(2,1)S(1)} %multiply_convert_fusion, bf16[512,1248]{1,0:T(8,128)(2,1)} %all-gather.2.cloned.1.call-done), kind=kOutput, calls=%fused_computation.30 | convolution fusion | flops 536870912 | bytes 3670016 | tf_op jit(solution)/shard_map/dot_general | solution.py:104
  98.7 3.5 %fusion.9 = f32[1024]{0:T(1024)S(1)} fusion(f32[512,1024]{1,0:T(8,128)S(1)} %fusion.20, bf16[1024,512]{0,1:T(8,128)(2,1)} %copy.78, f32[1024,512]{1,0:T(8,128)} %copy-done.1, bf16[512,128]{1,0:T(8,128)(2,1)S(1)} %copy-done, bf16[512,1248]{1,0:T(8,128)(2,1)} %all-gather.2.cloned.1.call-done, f32[128]{0:T(128)S(1)} %copy-done.5, f32[1024]{0:T(1024)S(1)} %get-tuple-element.23), kind=kOutput, calls=%fused_computation.18 | convolution fusion | flops 678689792 | bytes 5906944 | tf_op jit(solution)/shard_map/dot_general | solution.py:78
  102.5 6.0 %scatter_custom_fusion = f32[3,224]{0,1:T(8,128)S(1)} fusion(s32[1024]{0:T(1024)S(1)} %bitcast.84, f32[1024,3]{1,0:T(8,128)S(1)} %copy.83, f32[]{:T(128)} %constant.45.clone.1), kind=kCustom, calls=%fused_computation.43 | custom fusion | flops 3072 | bytes 2692 | tf_op jit(solution)/shard_map/scatter-add | solution.py:110
  108.7 0.7 fusion.38
  109.7 0.7 broadcast_in_dim.7
  110.3 3.7 %all-to-all-start = ((f32[8,1,1824]{2,1,0:T(1,128)}), f32[8,1,1824]{2,1,0:T(1,128)S(1)}, u32[]{:S(2)}, u32[]{:S(2)}) async-start(f32[8,1,1824]{2,1,0:T(1,128)} %broadcast_in_dim.7), calls=%async_computation | async-start | bytes 122880 | tf_op jit(solution)/shard_map/all_to_all | solution.py:37
  114.2 9.0 %all-to-all-done = f32[8,1,1824]{2,1,0:T(1,128)S(1)} async-done(((f32[8,1,1824]{2,1,0:T(1,128)}), f32[8,1,1824]{2,1,0:T(1,128)S(1)}, u32[]{:S(2)}, u32[]{:S(2)}) %all-to-all-start) | async-done | bytes 58400 | tf_op jit(solution)/shard_map/all_to_all | solution.py:37
  123.6 6.9 %collective-permute-start.5 = (f32[3,48]{1,0:T(4,128)S(1)}, f32[3,48]{1,0:T(4,128)S(1)}, u32[]{:S(2)}, u32[]{:S(2)}) collective-permute-start(f32[3,48]{1,0:T(4,128)S(1)} %get-tuple-element.21), channel_id=1, source_target_pairs={{8,0},{16,8},{24,16},{32,24},{40,32},{48,40},{56,48},{64,56},{72,6... | collective-permute-start | bytes 1736 | tf_op jit(solution)/shard_map/ppermute | solution.py:57
  130.4 2.6 %collective-permute-start.4 = (f32[3,48]{1,0:T(4,128)S(1)}, f32[3,48]{1,0:T(4,128)S(1)}, u32[]{:S(2)}, u32[]{:S(2)}) collective-permute-start(f32[3,48]{1,0:T(4,128)S(1)} %get-tuple-element.20), channel_id=1, source_target_pairs={{0,8},{8,16},{16,24},{24,32},{32,40},{40,48},{48,56},{56,64},{64,7... | collective-permute-start | bytes 1736 | tf_op jit(solution)/shard_map/ppermute | solution.py:57
  133.2 0.6 broadcast_in_dim.8
  133.8 7.3 %all-to-all-start.1 = ((f32[32,1,320]{2,1,0:T(1,128)}), f32[32,1,320]{2,1,0:T(1,128)S(1)}, u32[]{:S(2)}, u32[]{:S(2)}) async-start(f32[32,1,320]{2,1,0:T(1,128)} %broadcast_in_dim.8), calls=%async_computation.1 | async-start | bytes 98304 | tf_op jit(solution)/shard_map/all_to_all | solution.py:37
  141.2 0.7 fusion.46
  141.9 7.0 %all-to-all-done.1 = f32[32,1,320]{2,1,0:T(1,128)S(1)} async-done(((f32[32,1,320]{2,1,0:T(1,128)}), f32[32,1,320]{2,1,0:T(1,128)S(1)}, u32[]{:S(2)}, u32[]{:S(2)}) %all-to-all-start.1) | async-done | bytes 40992 | tf_op jit(solution)/shard_map/all_to_all | solution.py:37
  (55 shorter events, 3.3 us)
Async XLA Ops:
  7.2 26.4 %copy-start = (bf16[512,128]{1,0:T(8,128)(2,1)S(1)}, bf16[512,128]{1,0:T(8,128)(2,1)}, u32[]{:S(2)}) copy-start(bf16[512,128]{1,0:T(8,128)(2,1)} %param.16) | copy-start | bytes 393220
  7.2 79.5 %all-gather.2.cloned.1.call-start = ((), (), s32[]{:S(2)}) async-start(), calls=%async_computation.2 | async-start | bytes 1474560 | tf_op jit(solution)/shard_map/all_gather | solution.py:27
  8.1 6.9 %collective-permute-start = (bf16[64,48]{1,0:T(8,128)(2,1)S(1)}, bf16[64,48]{1,0:T(8,128)(2,1)S(1)}, u32[]{:S(2)}, u32[]{:S(2)}) collective-permute-start(bf16[64,48]{1,0:T(8,128)(2,1)S(1)} %get-tuple-element.19), channel_id=1, source_target_pairs={{0,8},{8,16},{16,24},{24,32},{32,40},{40,48},{48,56},{56,64},{64,7... | collective-permute-start | bytes 18440 | tf_op jit(solution)/shard_map/ppermute | solution.py:18
  13.0 5.1 %collective-permute-start.1 = (bf16[64,48]{1,0:T(8,128)(2,1)S(1)}, bf16[64,48]{1,0:T(8,128)(2,1)S(1)}, u32[]{:S(2)}, u32[]{:S(2)}) collective-permute-start(bf16[64,48]{1,0:T(8,128)(2,1)S(1)} %get-tuple-element.18), channel_id=1, source_target_pairs={{8,0},{16,8},{24,16},{32,24},{40,32},{48,40},{56,48},{64,56},{72,6... | collective-permute-start | bytes 18440 | tf_op jit(solution)/shard_map/ppermute | solution.py:19
  20.6 9.0 %collective-permute-start.3 = (f32[3,48]{1,0:T(4,128)S(1)}, f32[3,48]{1,0:T(4,128)S(1)}, u32[]{:S(2)}, u32[]{:S(2)}) collective-permute-start(f32[3,48]{1,0:T(4,128)S(1)} %get-tuple-element.25), channel_id=1, source_target_pairs={{8,0},{16,8},{24,16},{32,24},{40,32},{48,40},{56,48},{64,56},{72,6... | collective-permute-start | bytes 1736 | tf_op jit(solution)/shard_map/ppermute | solution.py:19
  22.6 7.1 %collective-permute-start.2 = (f32[3,48]{1,0:T(4,128)S(1)}, f32[3,48]{1,0:T(4,128)S(1)}, u32[]{:S(2)}, u32[]{:S(2)}) collective-permute-start(f32[3,48]{1,0:T(4,128)S(1)} %get-tuple-element.24), channel_id=1, source_target_pairs={{0,8},{8,16},{16,24},{24,32},{32,40},{40,48},{48,56},{56,64},{64,7... | collective-permute-start | bytes 1736 | tf_op jit(solution)/shard_map/ppermute | solution.py:18
  28.9 5.2 %copy-start.4 = (f32[128]{0:T(128)}, f32[128]{0:T(128)S(1)}, u32[]{:S(2)}) copy-start(f32[128]{0:T(128)S(1)} %convert_multiply_fusion) | copy-start | bytes 1540
  34.1 59.0 %copy-start.1 = (f32[1024,512]{1,0:T(8,128)}, f32[1024,512]{1,0:T(8,128)S(1)}, u32[]{:S(2)}) copy-start(f32[1024,512]{1,0:T(8,128)S(1)} %fusion.25) | copy-start | bytes 6291460
  91.8 1.4 copy-start.3
  91.8 1.4 copy-start.7
  96.8 1.9 %copy-start.5 = (f32[128]{0:T(128)S(1)}, f32[128]{0:T(128)}, u32[]{:S(2)}) copy-start(f32[128]{0:T(128)} %copy-done.4) | copy-start | bytes 1540
  98.7 9.9 %copy-start.2 = (f32[3,128]{1,0:T(4,128)S(1)}, f32[3,128]{1,0:T(4,128)}, u32[]{:S(2)}) copy-start(f32[3,128]{1,0:T(4,128)} %param.11) | copy-start | bytes 4612
  98.7 15.4 %copy-start.6 = (s32[128]{0:T(128)S(1)}, s32[128]{0:T(128)}, u32[]{:S(2)}) copy-start(s32[128]{0:T(128)} %param.13) | copy-start | bytes 1540
  110.3 12.8 %all-to-all-start = ((f32[8,1,1824]{2,1,0:T(1,128)}), f32[8,1,1824]{2,1,0:T(1,128)S(1)}, u32[]{:S(2)}, u32[]{:S(2)}) async-start(f32[8,1,1824]{2,1,0:T(1,128)} %broadcast_in_dim.7), calls=%async_computation | async-start | bytes 122880 | tf_op jit(solution)/shard_map/all_to_all | solution.py:37
  123.6 17.6 %collective-permute-start.5 = (f32[3,48]{1,0:T(4,128)S(1)}, f32[3,48]{1,0:T(4,128)S(1)}, u32[]{:S(2)}, u32[]{:S(2)}) collective-permute-start(f32[3,48]{1,0:T(4,128)S(1)} %get-tuple-element.21), channel_id=1, source_target_pairs={{8,0},{16,8},{24,16},{32,24},{40,32},{48,40},{56,48},{64,56},{72,6... | collective-permute-start | bytes 1736 | tf_op jit(solution)/shard_map/ppermute | solution.py:57
  130.4 10.8 %collective-permute-start.4 = (f32[3,48]{1,0:T(4,128)S(1)}, f32[3,48]{1,0:T(4,128)S(1)}, u32[]{:S(2)}, u32[]{:S(2)}) collective-permute-start(f32[3,48]{1,0:T(4,128)S(1)} %get-tuple-element.20), channel_id=1, source_target_pairs={{0,8},{8,16},{16,24},{24,32},{32,40},{40,48},{48,56},{56,64},{64,7... | collective-permute-start | bytes 1736 | tf_op jit(solution)/shard_map/ppermute | solution.py:57
  133.8 15.0 %all-to-all-start.1 = ((f32[32,1,320]{2,1,0:T(1,128)}), f32[32,1,320]{2,1,0:T(1,128)S(1)}, u32[]{:S(2)}, u32[]{:S(2)}) async-start(f32[32,1,320]{2,1,0:T(1,128)} %broadcast_in_dim.8), calls=%async_computation.1 | async-start | bytes 98304 | tf_op jit(solution)/shard_map/all_to_all | solution.py:37
Sparse Core Ops, SparseCore 0:
  19.9 66.7 all-gather.1
where the time goes:
time: 157 us
  waiting for transfers between devices  71.6 us (46%)
  starting transfers between devices  32.9 us (21%)
  local copies, waits for them, and re-layouts  15.9 us (10%)
  between operations  14.4 us (9%)
  other arithmetic  12 us (8%)
  matrix products  9.72 us (6%)
    all_gather x1, waiting for transfers between devices, turned_gather(): result, at, outs = (lax.all_gather(both, axis, axis=0, tiled=True), 0, [])  52.5 us
    all_to_all x2, waiting for transfers between devices, sent_to_all(): return lax.all_to_all(copies, axis, split_axis=0, concat_axis=0, tiled=True)  16 us
    all_to_all x2, starting transfers between devices, sent_to_all(): return lax.all_to_all(copies, axis, split_axis=0, concat_axis=0, tiled=True)  11.1 us
    ppermute x2, starting transfers between devices, from_behind(): return lax.ppermute(value, axis, pairs)  9.46 us
    ppermute x2, starting transfers between devices, with_halo(): before = lax.ppermute(last, axis, up)  8.56 us
    scatter-add x1, other arithmetic, local(): jnp.zeros((3, atom_count + 2 * RIM), jnp.float32).at[:, flat_index]  6.03 us
    gather x2, local copies, waits for them, and re-layouts, local(): far_feat = whole_feat[:, flat_index]  5.3 us
    ppermute x2, starting transfers between devices, with_halo(): after = lax.ppermute(first, axis, down)  3.83 us
  transfers between devices with their start and end apart: 9, of which 4 were waited for; matrix products, arithmetic and copies ran while one was open for 7% of the time, Pallas kernels for 0%

commit v1 on v0

--- a/solution.py
+++ b/solution.py
@@ -6,6 +6,13 @@
 RIM = 48
 sharpness = 40.0
 reach = 10.0
+
+
+def exchange_gather(x, axis, dim):
+    size = lax.axis_size(axis)
+    parts = jnp.stack([x for _ in range(size)])
+    parts = lax.all_to_all(parts, axis, split_axis=0, concat_axis=0)
+    return jnp.concatenate(parts, axis=dim)
 
 
 def with_halo(value, sides, width):
@@ -24,7 +31,7 @@
 def turned_gather(arrays, axis, dims):
     turned = [jnp.moveaxis(a, dim, 0) for a, dim in zip(arrays, dims)]
     both = jnp.concatenate([t.reshape(len(t), -1) for t in turned], axis=1)
-    result, at, outs = (lax.all_gather(both, axis, axis=0, tiled=True), 0, [])
+    result, at, outs = (exchange_gather(both, axis, 0), 0, [])
     for t, dim in zip(turned, dims):
         share = result[:, at : at + t[0].size].reshape(-1, *t.shape[1:])
         outs.append(jnp.moveaxis(share, 0, dim))

time: 157 us -> 128 us (0.82)
  waiting for transfers between devices: 71.6 us -> 39.9 us
  between operations: 14.4 us -> 0.91 us
  starting transfers between devices: 32.9 us -> 44.1 us
  matrix products: 9.72 us -> 13.2 us
  other arithmetic: 12 us -> 15.2 us
  local copies, waits for them, and re-layouts: 15.9 us -> 14.1 us
    all_gather x1 -> x0, waiting for transfers between devices: 52.5 us -> none  [turned_gather(): result, at, outs = (lax.all_gather(both, axis, axis=0, tiled=True), 0, [])]
    ppermute x2, waiting for transfers between devices: 3.12 us -> 24.6 us  [with_halo(): after = lax.ppermute(first, axis, down)]
    all_to_all x0 -> x1, starting transfers between devices: none -> 9.92 us  [exchange_gather(): parts = lax.all_to_all(parts, axis, split_axis=0, concat_axis=0)]
    all_to_all x2, starting transfers between devices: 11.1 us -> 16.3 us  [sent_to_all(): return lax.all_to_all(copies, axis, split_axis=0, concat_axis=0, tiled=True)]
    ppermute x2, starting transfers between devices: 9.46 us -> 5.56 us  [from_behind(): return lax.ppermute(value, axis, pairs)]
  transfers between devices with their start and end apart: 9 -> 9, of which waited for: 4 -> 4; matrix products, arithmetic and copies ran while one was open for 7% -> 9% of each run, Pallas kernels for 0% -> 0%
where the time goes in v1:
time: 128 us; the launch traced here: 127 us
  starting transfers between devices  44.1 us (34%)
  waiting for transfers between devices  39.9 us (31%)
  other arithmetic  15.2 us (12%)
  local copies, waits for them, and re-layouts  14.1 us (11%)
  matrix products  13.2 us (10%)
    ppermute x2, waiting for transfers between devices, with_halo(): after = lax.ppermute(first, axis, down)  24.6 us
    all_to_all x2, starting transfers between devices, sent_to_all(): return lax.all_to_all(copies, axis, split_axis=0, concat_axis=0, tiled=True)  16.3 us
    all_to_all x2, waiting for transfers between devices, sent_to_all(): return lax.all_to_all(copies, axis, split_axis=0, concat_axis=0, tiled=True)  15.3 us
    all_to_all x1, starting transfers between devices, exchange_gather(): parts = lax.all_to_all(parts, axis, split_axis=0, concat_axis=0)  9.92 us
    ppermute x2, starting transfers between devices, with_halo(): before = lax.ppermute(last, axis, up)  8.56 us
    scatter-add x1, other arithmetic, local(): jnp.zeros((3, atom_count + 2 * RIM), jnp.float32).at[:, flat_index]  6.16 us
    ppermute x2, starting transfers between devices, from_behind(): return lax.ppermute(value, axis, pairs)  5.56 us
    dot_general x1, matrix products, local(): mixed = jnp.dot(whole_mix, message, preferred_element_type=jnp.float32)  4.61 us
  transfers between devices with their start and end apart: 9, of which 4 were waited for; matrix products, arithmetic and copies ran while one was open for 9% of the time, Pallas kernels for 0%

profile of v1, /device:TPU:1, one launch (start us, length us, event | category | flops | bytes accessed | tf_op | source)
XLA Modules:
  0.0 127.5 jit_solution(1957305308297885416)
XLA Ops:
  0.6 0.9 fusion.56
  1.5 4.9 %collective-permute-start = (bf16[64,48]{1,0:T(8,128)(2,1)S(1)}, bf16[64,48]{1,0:T(8,128)(2,1)S(1)}, u32[]{:S(2)}, u32[]{:S(2)}) collective-permute-start(bf16[64,48]{1,0:T(8,128)(2,1)S(1)} %get-tuple-element.19), channel_id=1, source_target_pairs={{0,8},{8,16},{16,24},{24,32},{32,40},{40,48},{48,56},{56,64},{64,7... | collective-permute-start | bytes 18440 | tf_op jit(solution)/shard_map/ppermute | solution.py:25
  6.4 1.9 %collective-permute-start.1 = (bf16[64,48]{1,0:T(8,128)(2,1)S(1)}, bf16[64,48]{1,0:T(8,128)(2,1)S(1)}, u32[]{:S(2)}, u32[]{:S(2)}) collective-permute-start(bf16[64,48]{1,0:T(8,128)(2,1)S(1)} %get-tuple-element.18), channel_id=1, source_target_pairs={{8,0},{16,8},{24,16},{32,24},{40,32},{48,40},{56,48},{64,56},{72,6... | collective-permute-start | bytes 18440 | tf_op jit(solution)/shard_map/ppermute | solution.py:26
  8.4 3.1 %collective-permute-done.1 = bf16[64,48]{1,0:T(8,128)(2,1)S(1)} collective-permute-done((bf16[64,48]{1,0:T(8,128)(2,1)S(1)}, bf16[64,48]{1,0:T(8,128)(2,1)S(1)}, u32[]{:S(2)}, u32[]{:S(2)}) %collective-permute-start.1) | collective-permute-done | bytes 6176 | tf_op jit(solution)/shard_map/ppermute | solution.py:26
  11.5 1.0 concatenate.17
  12.6 1.1 stack.2
  13.7 9.9 %all-to-all-start = ((bf16[8,64,1248]{2,1,0:T(8,128)(2,1)}), bf16[8,64,1248]{2,1,0:T(8,128)(2,1)S(1)}, u32[]{:S(2)}, u32[]{:S(2)}) async-start(bf16[8,64,1248]{2,1,0:T(8,128)(2,1)} %stack.2), calls=%async_computation | async-start | bytes 2621440 | tf_op jit(solution)/shard_map/all_to_all | solution.py:14
  23.7 1.9 %collective-permute-start.3 = (f32[3,48]{1,0:T(4,128)S(1)}, f32[3,48]{1,0:T(4,128)S(1)}, u32[]{:S(2)}, u32[]{:S(2)}) collective-permute-start(f32[3,48]{1,0:T(4,128)S(1)} %get-tuple-element.25), channel_id=1, source_target_pairs={{8,0},{16,8},{24,16},{32,24},{40,32},{48,40},{56,48},{64,56},{72,6... | collective-permute-start | bytes 1736 | tf_op jit(solution)/shard_map/ppermute | solution.py:26
  25.6 3.6 %collective-permute-start.2 = (f32[3,48]{1,0:T(4,128)S(1)}, f32[3,48]{1,0:T(4,128)S(1)}, u32[]{:S(2)}, u32[]{:S(2)}) collective-permute-start(f32[3,48]{1,0:T(4,128)S(1)} %get-tuple-element.24), channel_id=1, source_target_pairs={{0,8},{8,16},{16,24},{24,32},{32,40},{40,48},{48,56},{56,64},{64,7... | collective-permute-start | bytes 1736 | tf_op jit(solution)/shard_map/ppermute | solution.py:25
  29.3 0.7 dynamic-slice_add_fusion
  30.0 1.3 %convert_bitcast_fusion = f32[1024]{0:T(1024)} fusion(s32[64,128]{1,0:T(8,128)} %param.15, s32[]{:T(128)S(6)} %select_n.16), kind=kLoop, calls=%fused_computation.65 | loop fusion | flops 1024 | bytes 8196 | tf_op jit(solution)/shard_map/convert_element_type | solution.py:106
  31.9 21.5 %collective-permute-done.3 = f32[3,48]{1,0:T(4,128)S(1)} collective-permute-done((f32[3,48]{1,0:T(4,128)S(1)}, f32[3,48]{1,0:T(4,128)S(1)}, u32[]{:S(2)}, u32[]{:S(2)}) %collective-permute-start.3) | collective-permute-done | bytes 608 | tf_op jit(solution)/shard_map/ppermute | solution.py:26
  53.6 2.8 %gather_fusion.1 = f32[1024,3]{1,0:T(8,128)S(1)} fusion(f32[3,224]{0,1:T(8,128)S(1)} %copy.73, s32[1024]{0:T(1024)S(1)} %broadcast_clamp_fusion), kind=kCustom, calls=%fused_computation.1 | custom fusion | bytes 28672 | tf_op jit(solution)/shard_map/gather | solution.py:105
  57.8 1.9 %fusion.25 = f32[1024,512]{1,0:T(8,128)} fusion(bf16[512,128]{1,0:T(8,128)(2,1)S(1)} %copy-done, f32[128]{0:T(128)S(1)} %convert_multiply_fusion, f32[1024]{0:T(1024)S(1)} %get-tuple-element.23), kind=kOutput, calls=%fused_computation.33 | convolution fusion | flops 134742016 | bytes 2232832 | tf_op jit(solution)/shard_map/dot_general | solution.py:80
  59.9 4.0 %gather_fusion = bf16[1024,512]{1,0:T(8,128)(2,1)S(1)} fusion(bf16[512,224]{0,1:T(8,128)(2,1)S(1)} %copy.85, s32[1024]{0:T(1024)S(1)} %broadcast_clamp_fusion), kind=kCustom, calls=%fused_computation | custom fusion | bytes 2101248 | tf_op jit(solution)/shard_map/gather | solution.py:104
  64.4 1.0 copy-done.1
  65.4 4.6 %multiply_convert_fusion = bf16[512,1024]{0,1:T(8,128)(2,1)} fusion(bf16[1024,512]{0,1:T(8,128)(2,1)S(1)} %copy.72, f32[1024,512]{1,0:T(8,128)} %fusion.25, f32[512]{0:T(512)} %param.19, f32[1024]{0:T(1024)} %convert_bitcast_fusion, bf16[512,1248]{1,0:T(8,128)(2,1)S(1)} %bitcast.81), kind=kOutput, calls=%fused_computation.19 | convolution fusion | flops 1083179008 | bytes 5249024 | tf_op jit(solution)/shard_map/dot_general | solution.py:109
  70.0 2.0 %fusion.20 = f32[512,1024]{1,0:T(8,128)S(1)} fusion(bf16[512,1024]{0,1:T(8,128)(2,1)} %multiply_convert_fusion, bf16[512,1248]{1,0:T(8,128)(2,1)S(1)} %bitcast.82), kind=kOutput, calls=%fused_computation.30 | convolution fusion | flops 536870912 | bytes 3670016 | tf_op jit(solution)/shard_map/dot_general | solution.py:111
  72.0 3.9 %fusion.9 = f32[1024]{0:T(1024)} fusion(f32[512,1024]{1,0:T(8,128)S(1)} %fusion.20, bf16[1024,512]{0,1:T(8,128)(2,1)} %copy-done.1, f32[1024,512]{1,0:T(8,128)} %fusion.25, bf16[512,128]{1,0:T(8,128)(2,1)S(1)} %copy-done, bf16[512,1248]{1,0:T(8,128)(2,1)S(1)} %bitcast.83, f32[128]{0:T(128)} %copy-done.5, f32[1024]{0:T(1024)} %copy-done.3), kind=kOutput, calls=%fused_computation.18 | convolution fusion | flops 678689792 | bytes 5906944 | tf_op jit(solution)/shard_map/dot_general | solution.py:85
  75.9 0.7 negate_bitcast_fusion
  76.7 0.7 broadcast_multiply_fusion
  77.7 6.2 %scatter_custom_fusion = f32[3,224]{0,1:T(8,128)S(1)} fusion(s32[1024]{0:T(1024)} %bitcast.89, f32[1024,3]{1,0:T(8,128)S(1)} %copy.77, f32[]{:T(128)} %constant.45.clone.1), kind=kCustom, calls=%fused_computation.43 | custom fusion | flops 3072 | bytes 3200 | tf_op jit(solution)/shard_map/scatter-add | solution.py:117
  83.8 0.7 fusion.44
  85.5 0.7 broadcast_in_dim.7
  86.2 9.3 %all-to-all-start.1 = ((f32[8,1,1824]{2,1,0:T(1,128)}), f32[8,1,1824]{2,1,0:T(1,128)S(1)}, u32[]{:S(2)}, u32[]{:S(2)}) async-start(f32[8,1,1824]{2,1,0:T(1,128)} %broadcast_in_dim.7), calls=%async_computation.1 | async-start | bytes 122880 | tf_op jit(solution)/shard_map/all_to_all | solution.py:44
  95.5 0.8 convert_reduce_fusion
  96.2 8.3 %all-to-all-done.1 = f32[8,1,1824]{2,1,0:T(1,128)S(1)} async-done(((f32[8,1,1824]{2,1,0:T(1,128)}), f32[8,1,1824]{2,1,0:T(1,128)S(1)}, u32[]{:S(2)}, u32[]{:S(2)}) %all-to-all-start.1) | async-done | bytes 58400 | tf_op jit(solution)/shard_map/all_to_all | solution.py:44
  104.6 0.8 fusion.41
  105.6 1.9 %collective-permute-start.5 = (f32[3,48]{1,0:T(4,128)S(1)}, f32[3,48]{1,0:T(4,128)S(1)}, u32[]{:S(2)}, u32[]{:S(2)}) collective-permute-start(f32[3,48]{1,0:T(4,128)S(1)} %get-tuple-element.21), channel_id=1, source_target_pairs={{8,0},{16,8},{24,16},{32,24},{40,32},{48,40},{56,48},{64,56},{72,6... | collective-permute-start | bytes 1736 | tf_op jit(solution)/shard_map/ppermute | solution.py:64
  107.5 3.6 %collective-permute-start.4 = (f32[3,48]{1,0:T(4,128)S(1)}, f32[3,48]{1,0:T(4,128)S(1)}, u32[]{:S(2)}, u32[]{:S(2)}) collective-permute-start(f32[3,48]{1,0:T(4,128)S(1)} %get-tuple-element.20), channel_id=1, source_target_pairs={{0,8},{8,16},{16,24},{24,32},{32,40},{40,48},{48,56},{56,64},{64,7... | collective-permute-start | bytes 1736 | tf_op jit(solution)/shard_map/ppermute | solution.py:64
  112.0 7.0 %all-to-all-start.2 = ((f32[32,1,320]{2,1,0:T(1,128)}), f32[32,1,320]{2,1,0:T(1,128)S(1)}, u32[]{:S(2)}, u32[]{:S(2)}) async-start(f32[32,1,320]{2,1,0:T(1,128)} %broadcast_in_dim.8), calls=%async_computation.2 | async-start | bytes 98304 | tf_op jit(solution)/shard_map/all_to_all | solution.py:44
  119.7 7.0 %all-to-all-done.2 = f32[32,1,320]{2,1,0:T(1,128)S(1)} async-done(((f32[32,1,320]{2,1,0:T(1,128)}), f32[32,1,320]{2,1,0:T(1,128)S(1)}, u32[]{:S(2)}, u32[]{:S(2)}) %all-to-all-start.2) | async-done | bytes 40992 | tf_op jit(solution)/shard_map/all_to_all | solution.py:44
  (51 shorter events, 6.8 us)
Async XLA Ops:
  0.6 57.2 %copy-start = (bf16[512,128]{1,0:T(8,128)(2,1)S(1)}, bf16[512,128]{1,0:T(8,128)(2,1)}, u32[]{:S(2)}) copy-start(bf16[512,128]{1,0:T(8,128)(2,1)} %param.16) | copy-start | bytes 393220
  1.5 6.9 %collective-permute-start = (bf16[64,48]{1,0:T(8,128)(2,1)S(1)}, bf16[64,48]{1,0:T(8,128)(2,1)S(1)}, u32[]{:S(2)}, u32[]{:S(2)}) collective-permute-start(bf16[64,48]{1,0:T(8,128)(2,1)S(1)} %get-tuple-element.19), channel_id=1, source_target_pairs={{0,8},{8,16},{16,24},{24,32},{32,40},{40,48},{48,56},{56,64},{64,7... | collective-permute-start | bytes 18440 | tf_op jit(solution)/shard_map/ppermute | solution.py:25
  6.4 5.1 %collective-permute-start.1 = (bf16[64,48]{1,0:T(8,128)(2,1)S(1)}, bf16[64,48]{1,0:T(8,128)(2,1)S(1)}, u32[]{:S(2)}, u32[]{:S(2)}) collective-permute-start(bf16[64,48]{1,0:T(8,128)(2,1)S(1)} %get-tuple-element.18), channel_id=1, source_target_pairs={{8,0},{16,8},{24,16},{32,24},{40,32},{48,40},{56,48},{64,56},{72,6... | collective-permute-start | bytes 18440 | tf_op jit(solution)/shard_map/ppermute | solution.py:26
  12.5 11.1 %copy-start.2 = (f32[3,128]{1,0:T(4,128)S(1)}, f32[3,128]{1,0:T(4,128)}, u32[]{:S(2)}) copy-start(f32[3,128]{1,0:T(4,128)} %param.11) | copy-start | bytes 4612
  13.7 46.0 %all-to-all-start = ((bf16[8,64,1248]{2,1,0:T(8,128)(2,1)}), bf16[8,64,1248]{2,1,0:T(8,128)(2,1)S(1)}, u32[]{:S(2)}, u32[]{:S(2)}) async-start(bf16[8,64,1248]{2,1,0:T(8,128)(2,1)} %stack.2), calls=%async_computation | async-start | bytes 2621440 | tf_op jit(solution)/shard_map/all_to_all | solution.py:14
  23.7 29.7 %collective-permute-start.3 = (f32[3,48]{1,0:T(4,128)S(1)}, f32[3,48]{1,0:T(4,128)S(1)}, u32[]{:S(2)}, u32[]{:S(2)}) collective-permute-start(f32[3,48]{1,0:T(4,128)S(1)} %get-tuple-element.25), channel_id=1, source_target_pairs={{8,0},{16,8},{24,16},{32,24},{40,32},{48,40},{56,48},{64,56},{72,6... | collective-permute-start | bytes 1736 | tf_op jit(solution)/shard_map/ppermute | solution.py:26
  25.6 27.8 %collective-permute-start.2 = (f32[3,48]{1,0:T(4,128)S(1)}, f32[3,48]{1,0:T(4,128)S(1)}, u32[]{:S(2)}, u32[]{:S(2)}) collective-permute-start(f32[3,48]{1,0:T(4,128)S(1)} %get-tuple-element.24), channel_id=1, source_target_pairs={{0,8},{8,16},{16,24},{24,32},{32,40},{40,48},{48,56},{56,64},{64,7... | collective-permute-start | bytes 1736 | tf_op jit(solution)/shard_map/ppermute | solution.py:25
  31.2 22.2 %copy-start.4 = (s32[1024,1]{0,1:T(1,128)}, s32[1024,1]{0,1:T(1,128)S(1)}, u32[]{:S(2)}) copy-start(s32[1024,1]{0,1:T(1,128)S(1)} %compare_select_fusion) | copy-start | bytes 12292
  31.3 28.5 %copy-start.5 = (f32[128]{0:T(128)}, f32[128]{0:T(128)S(1)}, u32[]{:S(2)}) copy-start(f32[128]{0:T(128)S(1)} %convert_multiply_fusion) | copy-start | bytes 1540
  57.8 1.9 %copy-start.3 = (f32[1024]{0:T(1024)}, f32[1024]{0:T(1024)S(1)}, u32[]{:S(2)}) copy-start(f32[1024]{0:T(1024)S(1)} %get-tuple-element.23) | copy-start | bytes 12292
  64.4 1.0 copy-start.1
  86.2 18.4 %all-to-all-start.1 = ((f32[8,1,1824]{2,1,0:T(1,128)}), f32[8,1,1824]{2,1,0:T(1,128)S(1)}, u32[]{:S(2)}, u32[]{:S(2)}) async-start(f32[8,1,1824]{2,1,0:T(1,128)} %broadcast_in_dim.7), calls=%async_computation.1 | async-start | bytes 122880 | tf_op jit(solution)/shard_map/all_to_all | solution.py:44
  105.6 13.4 %collective-permute-start.5 = (f32[3,48]{1,0:T(4,128)S(1)}, f32[3,48]{1,0:T(4,128)S(1)}, u32[]{:S(2)}, u32[]{:S(2)}) collective-permute-start(f32[3,48]{1,0:T(4,128)S(1)} %get-tuple-element.21), channel_id=1, source_target_pairs={{8,0},{16,8},{24,16},{32,24},{40,32},{48,40},{56,48},{64,56},{72,6... | collective-permute-start | bytes 1736 | tf_op jit(solution)/shard_map/ppermute | solution.py:64
  107.5 11.5 %collective-permute-start.4 = (f32[3,48]{1,0:T(4,128)S(1)}, f32[3,48]{1,0:T(4,128)S(1)}, u32[]{:S(2)}, u32[]{:S(2)}) collective-permute-start(f32[3,48]{1,0:T(4,128)S(1)} %get-tuple-element.20), channel_id=1, source_target_pairs={{0,8},{8,16},{16,24},{24,32},{32,40},{40,48},{48,56},{56,64},{64,7... | collective-permute-start | bytes 1736 | tf_op jit(solution)/shard_map/ppermute | solution.py:64
  112.0 14.6 %all-to-all-start.2 = ((f32[32,1,320]{2,1,0:T(1,128)}), f32[32,1,320]{2,1,0:T(1,128)S(1)}, u32[]{:S(2)}, u32[]{:S(2)}) async-start(f32[32,1,320]{2,1,0:T(1,128)} %broadcast_in_dim.8), calls=%async_computation.2 | async-start | bytes 98304 | tf_op jit(solution)/shard_map/all_to_all | solution.py:44
